TPU v7x, 32 devices: a whole 2x2x4 slice. The times are simulated.
32 devices in a mesh: dp: 2 (over x), seq: 4 (over z), tensor: 4 (over y, core).
Axes of the slice: x: 2, y: 2, z: 4, core: 2. Of those that a mesh axis runs over, the one named last changes fastest.
Arguments:
- image_states: bfloat16 [2, 2048, 3072], P('dp', 'seq', 'tensor'), may hold values from -6 to 6
- text_states: bfloat16 [4, 256, 3072], P(None, 'seq', 'tensor'), may hold values from -6 to 6
- image_qkv: bfloat16 [3072, 3, 3072], P(None, None, 'tensor'), may hold values from -0.109375 to 0.109375
- text_qkv: bfloat16 [3072, 3, 3072], P(None, None, 'tensor'), may hold values from -0.109375 to 0.109375
- image_out: bfloat16 [3072, 3072], P('tensor'), may hold values from -0.109375 to 0.109375
- final_weight: bfloat16 [3072, 64], replicated, may hold values from -0.109375 to 0.109375
- query_gain: float32 [128], replicated, may hold values from 1.5 to 2.5
- key_gain: float32 [128], replicated, may hold values from 1.5 to 2.5
- modulation: float32 [10, 7, 3072], replicated, may hold values from -3 to 3
- latent: float32 [2, 2048, 64], P('dp', ('seq', 'tensor')), may hold values from -6 to 6
- old_velocity: bfloat16 [2, 2048, 64], P('dp', ('seq', 'tensor')), may hold values from -6 to 6
- rollout_noise: float32 [2, 2048, 64], P('dp', ('seq', 'tensor')), may hold values from -6 to 6
- group_ids: int32 [2], P('dp'), may hold values from 0 to 3
- text_lengths: int32 [4], replicated, may hold values from 64 to 256
- step_ids: int32 [2], P('dp'), may hold values from 0 to 9
Outputs:
- step_mean: float32 [2, 2048, 64], P('dp', ('seq', 'tensor'))
- log_ratio: float32 [2], P('dp')
All inputs are finite; a program needn't handle non-finite values.
Results may differ from a plain program's by a relative error of at most 0.0023.
Values may be sent and summed in bfloat16 or wider, within the bound.
A program may use at most 192 MiB of HBM per device.

v0:
```python
import math

import jax
import jax.numpy as jnp
from jax import lax
from jax.sharding import PartitionSpec as P

NORM_EPSILON = 1e-06
NOISE_LEVEL = 0.7


def layer_norm(values):
    row_mean = jnp.mean(values, axis=-1, keepdims=True)
    centred = values - row_mean
    row_var = jnp.mean(centred * centred, axis=-1, keepdims=True)
    return centred * lax.rsqrt(row_var + NORM_EPSILON)


def head_norm(values, gain_vector):
    mean_square = jnp.mean(values * values, axis=-1, keepdims=True)
    return (values * lax.rsqrt(mean_square + NORM_EPSILON) * gain_vector).astype(jnp.bfloat16)


def plan(step_values, total_steps):
    step_count = total_steps + 1.0
    flow_time = (total_steps - step_values.astype(jnp.float32)) / step_count
    step_delta = -1.0 / step_count
    noise_sigma = NOISE_LEVEL * jnp.sqrt(flow_time / (1.0 - flow_time))
    spread = noise_sigma * jnp.sqrt(1.0 / step_count)
    return (flow_time, step_delta, noise_sigma, spread)


def drift_mean(latent_state, velocity, flow_time, step_delta, noise_sigma):
    drift = velocity + noise_sigma * noise_sigma / (2.0 * flow_time) * (
        latent_state + (1.0 - flow_time) * velocity
    )
    return latent_state + drift * step_delta


def shards(
    image_states,
    text_states,
    image_qkv,
    text_qkv,
    image_out,
    final_weight,
    query_gain,
    key_gain,
    modulation,
    latent,
    old_velocity,
    rollout_noise,
    group_ids,
    text_lengths,
    step_ids,
):
    samples = image_states.shape[0]
    local_img = image_states.shape[1]
    local_txt = text_states.shape[1]
    prompts = text_states.shape[0]
    head_dim = query_gain.shape[0]
    model_width = image_qkv.shape[0]
    local_heads = image_qkv.shape[2] // head_dim
    total_steps = modulation.shape[0]
    row_count = local_img // lax.axis_size("tensor")
    tensor_slot = lax.axis_index("tensor")
    step_pick = (step_ids[:, None] == jnp.arange(total_steps, dtype=jnp.int32)[None, :]).astype(
        jnp.float32
    )
    modrows = jnp.dot(
        step_pick,
        modulation.reshape(total_steps, -1),
        precision=lax.Precision.HIGHEST,
        preferred_element_type=jnp.float32,
    ).reshape(samples, 7, model_width)
    group_pick = group_ids[:, None] == jnp.arange(prompts, dtype=jnp.int32)[None, :]
    text_local = (
        jnp.dot(
            group_pick.astype(jnp.bfloat16),
            text_states.reshape(prompts, -1),
            preferred_element_type=jnp.float32,
        )
        .astype(jnp.bfloat16)
        .reshape(samples, local_txt, -1)
    )
    lengths = jnp.sum(jnp.where(group_pick, text_lengths[None, :], 0), axis=1)
    image_full, text_full = (
        lax.all_gather(image_states, "tensor", axis=2, tiled=True),
        lax.all_gather(text_local, "tensor", axis=2, tiled=True),
    )
    image_f = image_full.astype(jnp.float32)
    normed_img = (
        layer_norm(image_f) * (1.0 + modrows[:, 1, None, :]) + modrows[:, 0, None, :]
    ).astype(jnp.bfloat16)
    normed_txt = (
        layer_norm(text_full.astype(jnp.float32)) * (1.0 + modrows[:, 4, None, :])
        + modrows[:, 3, None, :]
    ).astype(jnp.bfloat16)

    def project(normed, weight):
        projected = jnp.dot(
            normed.reshape(-1, model_width),
            weight.reshape(model_width, -1),
            preferred_element_type=jnp.float32,
        )
        return projected.reshape(samples, normed.shape[1], 3, local_heads, head_dim)

    qkv_img = project(normed_img, image_qkv)
    qkv_txt = project(normed_txt, text_qkv)
    queries = head_norm(qkv_img[:, :, 0], query_gain)
    key_rows = head_norm(
        jnp.concatenate([qkv_txt[:, :, 1], qkv_img[:, :, 1]], axis=1), key_gain
    ).reshape(samples, local_txt + local_img, -1)
    value_rows = (
        jnp.concatenate([qkv_txt[:, :, 2], qkv_img[:, :, 2]], axis=1)
        .astype(jnp.bfloat16)
        .reshape(samples, local_txt + local_img, -1)
    )
    text_pos = lax.axis_index("seq") * local_txt + jnp.arange(local_txt, dtype=jnp.int32)
    text_valid = text_pos[None, :] < lengths[:, None]
    key_valid = jnp.concatenate([text_valid, jnp.ones((samples, local_img), bool)], axis=1).astype(
        jnp.bfloat16
    )
    score_scale = 1.0 / math.sqrt(head_dim)
    key_piece = lax.all_gather(key_rows, "seq", axis=1, tiled=True).reshape(
        samples, -1, local_heads, head_dim
    )
    value_piece = lax.all_gather(value_rows, "seq", axis=1, tiled=True).reshape(
        samples, -1, local_heads, head_dim
    )
    valid_piece = lax.all_gather(key_valid, "seq", axis=1, tiled=True).astype(jnp.float32)
    scores = (
        jnp.einsum("sqhd,skhd->shqk", queries, key_piece, preferred_element_type=jnp.float32)
        * score_scale
    )
    weights = jnp.exp(scores) * valid_piece[:, None, None, :]
    denominator = jnp.sum(weights, axis=-1)
    numerator = jnp.einsum(
        "shqk,skhd->shqd",
        weights.astype(jnp.bfloat16),
        value_piece,
        preferred_element_type=jnp.float32,
    )
    numerator, denominator = (numerator, denominator)
    attended = (numerator / denominator[..., None]).astype(jnp.bfloat16)
    attended = jnp.transpose(attended, (2, 0, 1, 3)).reshape(
        local_img, samples, local_heads * head_dim
    )
    summed = lax.psum_scatter(
        jnp.einsum("tsk,kd->tsd", attended, image_out, preferred_element_type=jnp.float32).astype(
            jnp.bfloat16
        ),
        "tensor",
        scatter_dimension=0,
        tiled=True,
    ).astype(jnp.float32)
    summed = jnp.transpose(summed, (1, 0, 2))
    own_rows = lax.dynamic_slice_in_dim(image_f, tensor_slot * row_count, row_count, 1)
    resid = own_rows + modrows[:, 2, None, :] * summed
    final_normed = (
        layer_norm(resid) * (1.0 + modrows[:, 6, None, :]) + modrows[:, 5, None, :]
    ).astype(jnp.bfloat16)
    velocity = jnp.dot(
        final_normed.reshape(-1, model_width), final_weight, preferred_element_type=jnp.float32
    ).reshape(samples, row_count, -1)
    flow_time, step_delta, noise_sigma, spread = plan(step_ids, total_steps)
    flow_e = flow_time[:, None, None]
    sigma_e = noise_sigma[:, None, None]
    step_mean = drift_mean(latent, velocity, flow_e, step_delta, sigma_e)
    mean_old = drift_mean(latent, old_velocity.astype(jnp.float32), flow_e, step_delta, sigma_e)
    shifted = rollout_noise + (mean_old - step_mean) / spread[:, None, None]
    partial_ratio = jnp.sum(rollout_noise * rollout_noise - shifted * shifted, axis=(1, 2)) * 0.5
    ratio_total = lax.psum(partial_ratio, ("seq", "tensor"))
    elements = latent.shape[1] * lax.axis_size("seq") * lax.axis_size("tensor") * latent.shape[2]
    return (step_mean, ratio_total / elements)


def solution(mesh):
    placed = (
        P("dp", "seq", "tensor"),
        P(None, "seq", "tensor"),
        P(None, None, "tensor"),
        P(None, None, "tensor"),
        P("tensor", None),
        P(),
        P(),
        P(),
        P(),
        P("dp", ("seq", "tensor"), None),
        P("dp", ("seq", "tensor"), None),
        P("dp", ("seq", "tensor"), None),
        P("dp"),
        P(),
        P("dp"),
    )
    return jax.shard_map(
        shards,
        mesh=mesh,
        in_specs=placed,
        out_specs=(P("dp", ("seq", "tensor"), None), P("dp")),
        check_vma=False,
    )
```

profile of v0, /device:TPU:0, one launch (start us, length us, event | category | flops | bytes accessed | tf_op | source)
XLA Modules:
  0.0 343.8 jit_solution(12398797501671049936)
XLA Ops:
  11.2 18.8 %copy.35 = bf16[3072,3,768]{0,2,1:T(8,128)(2,1)} copy(bf16[3072,3,768]{2,0,1:T(8,128)(2,1)} %param.17) | data formatting | bytes 28311552 | tf_op args[2]
  31.5 18.8 %copy.36 = bf16[3072,3,768]{0,2,1:T(8,128)(2,1)} copy(bf16[3072,3,768]{2,0,1:T(8,128)(2,1)} %param.18) | data formatting | bytes 28311552 | tf_op args[3]
  50.2 8.1 %all_gather.16 = bf16[1,64,3072]{2,1,0:T(8,128)(2,1)S(1)} all-gather(bf16[1,64,768]{2,1,0:T(8,128)(2,1)S(1)} %reshape.497), channel_id=1, replica_groups=mesh['dp'=2,'seq'=4,'tensor'=4] {'tensor'}, dimensions={2}, use_global_device_ids=true | all-gather | bytes 491520 | tf_op jit(solution)/shard_map/all_gather | solution.py:89
  61.1 7.2 %convolution_bitcast_fusion = f32[1,64,3,6,128]{1,4,3,2,0:T(8,128)S(1)} fusion(bf16[3,6,128,3072]{3,2,1,0:T(8,128)(2,1)} %bitcast.158, bf16[1,64,3072]{2,1,0:T(8,128)(2,1)S(1)} %all_gather.16, f32[3072]{0:T(1024)S(1)} %bitcast.175, f32[3072]{0:T(1024)S(1)} %bitcast.174, f32[64]{0:T(128)S(1)} %add_rsqrt_fusion.4, f32[64]{0:T(128)S(1)} %broadcast_multiply_fusion.2), kind=kOutput, calls=%fused_computation.33 | convolution fusion | flops 907149312 | bytes 15163904 | tf_op jit(solution)/shard_map/dot_general | solution.py:101
  69.6 2.5 convert_reduce_fusion
  73.4 10.8 %fusion.14 = f32[1,512,3,6,128]{1,4,3,2,0:T(8,128)S(1)} fusion(bf16[3,6,128,3072]{3,2,1,0:T(8,128)(2,1)} %bitcast.160, bf16[1,512,3072]{2,1,0:T(8,128)(2,1)S(1)} %copy-done.1, f32[3072]{0:T(1024)S(1)} %bitcast.179, f32[3072]{0:T(1024)S(1)} %bitcast.178, f32[512]{0:T(512)S(1)} %add_rsqrt_fusion.2, f32[512]{0:T(512)S(1)} %broadcast_multiply_fusion), kind=kOutput, calls=%fused_computation.17 | convolution fusion | flops 7257194496 | bytes 22048768 | tf_op jit(solution)/shard_map/dot_general | solution.py:101
  88.7 2.2 copy.38
  94.4 2.4 slice.78
  96.8 2.3 copy.43
  99.1 2.2 pad_maximum_fusion
  104.1 13.2 %all-reduce.1 = bf16[2304]{0:T(1024)(128)(2,1)S(1)} all-reduce(bf16[2304]{0:T(1024)(128)(2,1)S(1)} %dynamic-update-slice), channel_id=1, replica_groups=mesh['dp'=2,'seq'=4,'tensor'=4] {'seq'}, use_global_device_ids=true, to_apply=%add.1 | all-reduce | flops 2304 | bytes 9216
  118.6 43.7 %all-gather.6.cloned.1.call-done = bf16[1,2304,768]{2,1,0:T(8,128)(2,1)} async-done(((bf16[1,576,768]{2,1,0:T(8,128)(2,1)}), bf16[1,2304,768]{2,1,0:T(8,128)(2,1)}) %all-gather.6.cloned.1.call-update) | async-done | bytes 3538960 | tf_op jit(solution)/shard_map/all_gather | solution.py:125
  162.3 5.8 %copy.39 = bf16[1,2304,768]{1,2,0:T(8,128)(2,1)} copy(bf16[1,2304,768]{2,1,0:T(8,128)(2,1)} %all-gather.6.cloned.1.call-done) | data formatting | bytes 7077888 | tf_op jit(solution)/shard_map/all_gather | solution.py:125
  168.1 15.9 %fusion = (f32[6,512]{1,0:T(8,128)}, f32[6,512,2304]{2,1,0:T(8,128)}) fusion(f32[2304]{0:T(1024)} %mul.326, bf16[2304,6,128]{0,2,1:T(8,128)(2,1)} %bitcast.159, f32[1,512,3,6,128]{1,4,3,2,0:T(8,128)} %copy-done.2, f32[128]{0:T(128)} %param.21, f32[512,6]{0,1:T(8,128)S(1)} %add_rsqrt_fusion.1), kind=kOutput, calls=%fused_computation.1 | convolution fusion | flops 1834349568 | bytes 33460736 | tf_op jit(solution)/shard_map/sqhd,skhd->shqk/dot_general | solution.py:133
  184.0 48.5 %all-gather.8.cloned.1.call-done = bf16[1,2304,768]{2,1,0:T(8,128)(2,1)} async-done(((bf16[1,576,768]{2,1,0:T(8,128)(2,1)}), bf16[1,2304,768]{2,1,0:T(8,128)(2,1)}) %all-gather.8.cloned.1.call-update) | async-done | bytes 3538960 | tf_op jit(solution)/shard_map/all_gather | solution.py:128
  232.5 5.8 %copy.44 = bf16[1,2304,768]{1,2,0:T(8,128)(2,1)} copy(bf16[1,2304,768]{2,1,0:T(8,128)(2,1)} %all-gather.8.cloned.1.call-done) | data formatting | bytes 7077888 | tf_op jit(solution)/shard_map/all_gather | solution.py:128
  238.3 12.9 %divide_convert_fusion = bf16[6,512,128]{1,2,0:T(8,128)(2,1)S(1)} fusion(bf16[2304,6,128]{0,2,1:T(8,128)(2,1)} %bitcast.164, f32[6,512,2304]{2,1,0:T(8,128)} %get-tuple-element.15, f32[2304]{0:T(1024)S(1)} %copy-done.9, f32[6,512]{1,0:T(8,128)} %get-tuple-element.14), kind=kOutput, calls=%fused_computation.31 | convolution fusion | flops 1833959424 | bytes 32658432 | tf_op jit(solution)/shard_map/shqk,skhd->shqd/dot_general | solution.py:138
  251.2 6.4 %fusion.6 = bf16[512,1,3072]{2,0,1:T(8,128)(2,1)} fusion(bf16[512,768]{0,1:T(8,128)(2,1)S(1)} %bitcast.180, bf16[768,3072]{1,0:T(8,128)(2,1)} %param.19), kind=kOutput, calls=%fused_computation.10 | convolution fusion | flops 2417491968 | bytes 8650752 | tf_op jit(solution)/shard_map/tsk,kd->tsd/dot_general | solution.py:150
  257.8 3.5 %convert_element_type.76 = f32[1,512,3072]{2,1,0:T(8,128)} convert(bf16[1,512,3072]{2,1,0:T(8,128)(2,1)S(1)} %copy-done.1) | non-fusion elementwise | flops 1572864 | bytes 9437184 | tf_op jit(solution)/shard_map/convert_element_type | solution.py:91
  261.3 33.0 %reduce-scatter.2.cloned.1.call-done = bf16[128,1,3072]{2,0,1:T(8,128)(2,1)} async-done(((bf16[512,1,3072]{2,0,1:T(8,128)(2,1)}), bf16[128,1,3072]{2,0,1:T(8,128)(2,1)}) %reduce-scatter.2.cloned.1.call-update) | async-done | bytes 786448 | tf_op jit(solution)/shard_map/reduce_scatter | solution.py:149
  294.3 2.0 fusion.47
  296.3 2.1 multiply_reduce_fusion.1
  298.5 3.2 fusion.63
  302.3 33.2 %psum.7 = f32[1]{0:T(128)} all-reduce(f32[1]{0:T(128)} %bitcast.53), channel_id=1, replica_groups=mesh['dp'=2,'seq'=4,'tensor'=4] {'seq','tensor'}, use_global_device_ids=true, to_apply=%region_12.13 | all-reduce | flops 1 | bytes 8 | tf_op jit(solution)/shard_map/psum | solution.py:173
  (82 shorter events, 20.9 us)
Async XLA Ops:
  7.2 291.2 %copy-start = (bf16[3072,64]{0,1:T(8,128)(2,1)S(1)}, bf16[3072,64]{0,1:T(8,128)(2,1)}, u32[]{:S(2)}) copy-start(bf16[3072,64]{0,1:T(8,128)(2,1)} %param.20) | copy-start | bytes 1179652
  7.2 62.4 %all-gather.4.cloned.1.call-start = ((), (), s32[]{:S(2)}) async-start(), calls=%async_computation.1 | async-start | bytes 3932160 | tf_op jit(solution)/shard_map/all_gather | solution.py:88
  7.9 154.4 %all-gather.6.cloned.1.call-start = ((), (), s32[]{:S(2)}) async-start(), calls=%async_computation.2 | async-start | bytes 4423680 | tf_op jit(solution)/shard_map/all_gather | solution.py:125
  11.2 19.4 %copy-start.7 = (bf16[4,64,768]{2,1,0:T(8,128)(2,1)S(1)}, bf16[4,64,768]{2,1,0:T(8,128)(2,1)}, u32[]{:S(2)}) copy-start(bf16[4,64,768]{2,1,0:T(8,128)(2,1)} %param.16) | copy-start | bytes 1179652
  31.4 27.4 %copy-start.13 = (f32[128]{0:T(128)S(1)}, f32[128]{0:T(128)}, u32[]{:S(2)}) copy-start(f32[128]{0:T(128)} %param.22) | copy-start | bytes 1540
  68.3 1.3 copy-start.4
  69.6 2.8 copy-start.1
  69.6 3.8 %copy-start.12 = (f32[1,1,3072]{2,0,1:T(1,128)S(1)}, f32[1,1,3072]{2,0,1:T(1,128)}, u32[]{:S(2)}) copy-start(f32[1,1,3072]{2,0,1:T(1,128)} %get-tuple-element.9) | copy-start | bytes 36868
  84.2 2.2 copy-start.2
  84.2 2.2 copy-start.6
  84.2 2.8 copy-start.5
  90.9 141.6 %all-gather.8.cloned.1.call-start = ((), (), s32[]{:S(2)}) async-start(), calls=%async_computation.3 | async-start | bytes 4423680 | tf_op jit(solution)/shard_map/all_gather | solution.py:128
  92.7 8.7 %copy-start.18 = (u32[32]{0:T(128)S(1)}, u32[32]{0:T(128)}, u32[]{:S(2)}) copy-start(u32[32]{0:T(128)} %constant.81) | copy-start | bytes 388
  92.7 9.9 %copy-start.17 = (s32[4]{0:T(128)S(1)}, s32[4]{0:T(128)}, u32[]{:S(2)}) copy-start(s32[4]{0:T(128)} %param.28) | copy-start | bytes 52
  101.3 193.0 %reduce-scatter.2.cloned.1.call-start = ((), (), s32[]{:S(2)}) async-start(), calls=%async_computation.4 | async-start | bytes 3932160 | tf_op jit(solution)/shard_map/reduce_scatter | solution.py:149
  184.0 54.3 %copy-start.9 = (f32[2304]{0:T(1024)S(1)}, f32[2304]{0:T(1024)}, u32[]{:S(2)}) copy-start(f32[2304]{0:T(1024)} %mul.326) | copy-start | bytes 27652
  257.8 36.5 %copy-start.8 = (f32[1,1,3072]{2,0,1:T(1,128)S(1)}, f32[1,1,3072]{2,0,1:T(1,128)}, u32[]{:S(2)}) copy-start(f32[1,1,3072]{2,0,1:T(1,128)} %get-tuple-element.7) | copy-start | bytes 36868
  261.3 37.1 %copy-start.10 = (f32[1,1,3072]{2,1,0:T(1,128)S(1)}, f32[1,1,3072]{2,1,0:T(1,128)}, u32[]{:S(2)}) copy-start(f32[1,1,3072]{2,1,0:T(1,128)} %get-tuple-element.12) | copy-start | bytes 36868
  261.3 37.1 %copy-start.11 = (f32[1,1,3072]{2,0,1:T(1,128)S(1)}, f32[1,1,3072]{2,0,1:T(1,128)}, u32[]{:S(2)}) copy-start(f32[1,1,3072]{2,0,1:T(1,128)} %get-tuple-element.10) | copy-start | bytes 36868
  261.3 37.2 %copy-start.14 = (f32[1,128,64]{1,2,0:T(8,128)S(1)}, f32[1,128,64]{1,2,0:T(8,128)}, u32[]{:S(2)}) copy-start(f32[1,128,64]{1,2,0:T(8,128)} %param.26) | copy-start | bytes 98308
  261.3 37.2 %copy-start.15 = (f32[1,128,64]{1,2,0:T(8,128)S(1)}, f32[1,128,64]{1,2,0:T(8,128)}, u32[]{:S(2)}) copy-start(f32[1,128,64]{1,2,0:T(8,128)} %param.24) | copy-start | bytes 98308
  261.3 37.2 %copy-start.16 = (bf16[1,128,64]{1,2,0:T(8,128)(2,1)S(1)}, bf16[1,128,64]{1,2,0:T(8,128)(2,1)}, u32[]{:S(2)}) copy-start(bf16[1,128,64]{1,2,0:T(8,128)(2,1)} %param.25) | copy-start | bytes 49156
  294.3 4.2 %copy-start.3 = (bf16[128,1,3072]{2,0,1:T(8,128)(2,1)S(1)}, bf16[128,1,3072]{2,0,1:T(8,128)(2,1)}, u32[]{:S(2)}) copy-start(bf16[128,1,3072]{2,0,1:T(8,128)(2,1)} %reduce-scatter.2.cloned.1.call-done) | copy-start | bytes 2359300
Sparse Core Ops, SparseCore 0:
  9.5 31.2 all-gather.3
  91.0 71.2 all-gather.5
  163.9 68.5 all-gather.7
  257.8 36.4 reduce-scatter.1
where the time goes:
time: 345 us; the launch traced here: 344 us
  waiting for transfers between devices  126 us (37%)
  local copies, waits for them, and re-layouts  66.6 us (19%)
  matrix products  57.8 us (17%)
  blocking collectives  54.5 us (16%)
  other arithmetic  20.3 us (6%)
  between operations  18.5 us (5%)
    all_gather x1, waiting for transfers between devices, shards(): lax.all_gather(value_rows, 'seq', axis=1, tiled=True)  48.5 us
    all_gather x1, waiting for transfers between devices, shards(): lax.all_gather(key_rows, 'seq', axis=1, tiled=True)  43.7 us
    unnamed x46, local copies, waits for them, and re-layouts  42.4 us
    psum x1, blocking collectives, shards(): ratio_total = lax.psum(partial_ratio, ('seq', 'tensor'))  33.2 us
    reduce_scatter x1, waiting for transfers between devices, shards(): lax.psum_scatter(jnp.einsum('tsk,kd->tsd', attended, image_out, preferred...  33 us
    dot_general x2, matrix products, project(): jnp.dot(normed.reshape(-1, model_width), weight.reshape(model_width, -1),...  18 us
    dot_general x1, matrix products, shards(): jnp.einsum('sqhd,skhd->shqk', queries, key_piece, preferred_element_type=...  15.9 us
    unnamed x1, blocking collectives  13.2 us
  transfers between devices with their start and end apart: 4, of which 3 were waited for; matrix products, arithmetic and copies ran while one was open for 26% of the time, Pallas kernels for 0%

commit v1 on v0

v1 whole, which is shorter than its diff:
```python
import functools
import math

import jax
import jax.numpy as jnp
from jax import lax
from jax.experimental import pallas as pl
from jax.experimental.pallas import tpu as pltpu
from jax.sharding import PartitionSpec as P

NORM_EPSILON = 1e-06
NOISE_LEVEL = 0.7


def layer_norm(values):
    row_mean = jnp.mean(values, axis=-1, keepdims=True)
    centred = values - row_mean
    row_var = jnp.mean(centred * centred, axis=-1, keepdims=True)
    return centred * lax.rsqrt(row_var + NORM_EPSILON)


def head_norm(values, gain_vector):
    mean_square = jnp.mean(values * values, axis=-1, keepdims=True)
    return (values * lax.rsqrt(mean_square + NORM_EPSILON) * gain_vector).astype(jnp.bfloat16)


def plan(step_values, total_steps):
    step_count = total_steps + 1.0
    flow_time = (total_steps - step_values.astype(jnp.float32)) / step_count
    step_delta = -1.0 / step_count
    noise_sigma = NOISE_LEVEL * jnp.sqrt(flow_time / (1.0 - flow_time))
    spread = noise_sigma * jnp.sqrt(1.0 / step_count)
    return (flow_time, step_delta, noise_sigma, spread)


def drift_mean(latent_state, velocity, flow_time, step_delta, noise_sigma):
    drift = velocity + noise_sigma * noise_sigma / (2.0 * flow_time) * (
        latent_state + (1.0 - flow_time) * velocity
    )
    return latent_state + drift * step_delta


MESH = pl.DeviceIdType.MESH
VMEM_LIMIT = 60 * 1024 * 1024


def first_head(rank, ranks, heads, odd):
    extra = heads % ranks
    base = heads // ranks
    even_start = base * rank + jnp.minimum(rank, extra)
    odd_start = base * rank + jnp.maximum(rank - (ranks - extra), 0)
    return jnp.where(odd == 1, odd_start, even_start)


def head_owner(head, ranks, heads, odd):
    owner = jnp.int32(0)
    for rank in range(1, ranks):
        owner = owner + (head >= first_head(jnp.int32(rank), ranks, heads, odd)).astype(jnp.int32)
    return owner, head - first_head(owner, ranks, heads, odd)


def meet(axis, size, me):
    barrier = pltpu.get_barrier_semaphore()
    for step in range(1, size):
        pl.semaphore_signal(
            barrier, inc=1, device_id={axis: lax.rem(me + step, size)}, device_id_type=MESH
        )
    pl.semaphore_wait(barrier, size - 1)


def project_kernel(
    ranks, heads, group, img_ref, txt_ref, wimg_ref, wtxt_ref, qgain_ref, kgain_ref,
    q_out, k_out, v_out, qbuf, kvbuf, send_sem, recv_sem, local_sem,
):
    me = lax.axis_index("seq")
    odd = lax.rem(lax.axis_index("tensor"), 2)
    step = pl.program_id(0)
    pieces = heads // group
    steps = 3 * pieces
    local_txt = txt_ref.shape[0]
    slots = q_out.shape[0]
    hd = qgain_ref.shape[1]
    dot = functools.partial(jnp.dot, preferred_element_type=jnp.float32)

    @pl.when(step == 0)
    def _():
        meet("seq", ranks, me)

    def normed(values, gain_ref):
        mean_square = jnp.mean(values * values, axis=-1, keepdims=True)
        return (values * lax.rsqrt(mean_square + NORM_EPSILON) * gain_ref[...]).astype(jnp.bfloat16)

    piece = lax.rem(step, pieces)
    kind = step // pieces
    img = dot(img_ref[...], wimg_ref[0])

    @pl.when(kind < 2)
    def _():
        txt = dot(txt_ref[...], wtxt_ref[0])
        for g in range(group):
            cols = slice(g * hd, (g + 1) * hd)
            head = kind * heads + piece * group + g

            @pl.when(kind == 0)
            def _():
                kvbuf[head, :local_txt, :] = normed(txt[:, cols], kgain_ref)
                kvbuf[head, local_txt:, :] = normed(img[:, cols], kgain_ref)

            @pl.when(kind == 1)
            def _():
                kvbuf[head, :local_txt, :] = txt[:, cols].astype(jnp.bfloat16)
                kvbuf[head, local_txt:, :] = img[:, cols].astype(jnp.bfloat16)

    @pl.when(kind == 2)
    def _():
        for g in range(group):
            qbuf[piece * group + g] = normed(img[:, g * hd : (g + 1) * hd], qgain_ref)

    def ship(which):
        kind_of = which // pieces
        for g in range(group):
            head = lax.rem(which, pieces) * group + g
            owner, slot = head_owner(head, ranks, heads, odd)
            for number, out in ((0, k_out), (1, v_out), (2, q_out)):
                source = qbuf.at[head] if number == 2 else kvbuf.at[number * heads + head]

                @pl.when((kind_of == number) & (owner == me))
                def _():
                    pltpu.make_async_copy(
                        source, out.at[slot, me], local_sem.at[number, slot]
                    ).start()

                @pl.when((kind_of == number) & (owner != me))
                def _():
                    pltpu.make_async_remote_copy(
                        src_ref=source,
                        dst_ref=out.at[slot, me],
                        send_sem=send_sem.at[number, head],
                        recv_sem=recv_sem.at[number, slot, me],
                        device_id={"seq": owner},
                        device_id_type=MESH,
                    ).start()

    @pl.when(step > 0)
    def _():
        ship(step - 1)

    @pl.when(step == steps - 1)
    def _():
        ship(step)
        mine = first_head(me + 1, ranks, heads, odd) - first_head(me, ranks, heads, odd)
        for number, out in ((0, k_out), (1, v_out), (2, q_out)):
            buf = qbuf if number == 2 else kvbuf

            for head in range(heads):
                owner, _ = head_owner(jnp.int32(head), ranks, heads, odd)

                @pl.when(owner != me)
                def _():
                    src = buf.at[head]
                    pltpu.make_async_remote_copy(
                        src_ref=src, dst_ref=out.at[0, me],
                        send_sem=send_sem.at[number, head], recv_sem=recv_sem.at[number, 0, me],
                        device_id={"seq": owner}, device_id_type=MESH,
                    ).wait_send()

            for slot in range(slots):
                @pl.when(slot < mine)
                def _():
                    pltpu.make_async_copy(
                        buf.at[0], out.at[slot, me], local_sem.at[number, slot]
                    ).wait()
                    for hop in range(1, ranks):
                        peer = lax.rem(me + hop, ranks)
                        pltpu.make_async_remote_copy(
                            src_ref=buf.at[0], dst_ref=out.at[slot, peer],
                            send_sem=send_sem.at[number, 0], recv_sem=recv_sem.at[number, slot, peer],
                            device_id={"seq": peer}, device_id_type=MESH,
                        ).wait_recv()


def project(ranks, heads, normed_img, normed_txt, wimg, wtxt, query_gain, key_gain):
    width = normed_img.shape[1]
    hd = query_gain.shape[0]
    group = 2 if heads % 2 == 0 else 1
    pieces = heads // group
    slots = -(-heads // ranks)
    local_img, local_txt = normed_img.shape[0], normed_txt.shape[0]
    rows = local_img + local_txt
    kv = jax.ShapeDtypeStruct((slots, ranks, rows, hd), jnp.bfloat16)
    whole = pl.BlockSpec(memory_space=pltpu.VMEM)
    return pl.pallas_call(
        functools.partial(project_kernel, ranks, heads, group),
        grid=(3 * pieces,),
        out_shape=(jax.ShapeDtypeStruct((slots, ranks, local_img, hd), jnp.bfloat16), kv, kv),
        in_specs=[
            whole,
            whole,
            pl.BlockSpec((1, width, group * hd), lambda i: ((i // pieces + 1) % 3, 0, i % pieces)),
            pl.BlockSpec(
                (1, width, group * hd),
                lambda i: (
                    jnp.minimum(i // pieces, 1), 0,
                    jnp.where(i < 2 * pieces, i % pieces, pieces - 1),
                ),
            ),
            whole,
            whole,
        ],
        out_specs=[pl.BlockSpec(memory_space=pl.ANY)] * 3,
        scratch_shapes=[
            pltpu.VMEM((heads, local_img, hd), jnp.bfloat16),
            pltpu.VMEM((2 * heads, rows, hd), jnp.bfloat16),
            pltpu.SemaphoreType.DMA((3, heads)),
            pltpu.SemaphoreType.DMA((3, slots, ranks)),
            pltpu.SemaphoreType.DMA((3, slots)),
        ],
        compiler_params=pltpu.CompilerParams(
            collective_id=0, has_side_effects=True, vmem_limit_bytes=VMEM_LIMIT,
            dimension_semantics=("arbitrary",),
        ),
    )(normed_img, normed_txt, wimg, wtxt, query_gain[None, :], key_gain[None, :])


def attend_kernel(
    ranks, heads, q_ref, k_ref, v_ref, valid_ref, out_ref, buf, send_sem, recv_sem, local_sem
):
    me = lax.axis_index("seq")
    odd = lax.rem(lax.axis_index("tensor"), 2)
    meet("seq", ranks, me)
    slots, _, local_img, hd = q_ref.shape
    start = first_head(me, ranks, heads, odd)
    mine = first_head(me + 1, ranks, heads, odd) - start
    scale = math.log2(math.e) / math.sqrt(hd)
    tile = min(256, local_img)

    def columns(head):
        return out_ref.at[:, pl.ds(pl.multiple_of(head * hd, hd), hd)]

    def back(peer, slot):
        return pltpu.make_async_remote_copy(
            src_ref=buf.at[slot, peer],
            dst_ref=columns(start + slot),
            send_sem=send_sem.at[slot, peer],
            recv_sem=recv_sem.at[start + slot],
            device_id={"seq": peer},
            device_id_type=MESH,
        )

    def place(number):
        return number // ranks, lax.rem(me + 1 + lax.rem(number, ranks), ranks)

    def ship(number):
        slot, peer = place(number)

        @pl.when((slot < mine) & (peer != me))
        def _():
            back(peer, slot).start()

        @pl.when((slot < mine) & (peer == me))
        def _():
            pltpu.make_async_copy(
                buf.at[slot, me], columns(start + slot), local_sem.at[slot]
            ).start()

    def one(number, carry):
        slot, peer = place(number)

        @pl.when(slot < mine)
        def _():
            for low in range(0, local_img, tile):
                queries = q_ref[slot, peer, low : low + tile, :]
                total = jnp.zeros((tile, hd), jnp.float32)
                denominator = jnp.zeros((tile, 1), jnp.float32)
                for block in range(ranks):
                    scores = lax.dot_general(
                        queries, k_ref[slot, block], (((1,), (1,)), ((), ())),
                        preferred_element_type=jnp.float32,
                    )
                    weights = jnp.exp2(scores * scale) * valid_ref[block]
                    denominator = denominator + jnp.sum(weights, axis=-1, keepdims=True)
                    total = total + jnp.dot(
                        weights.astype(jnp.bfloat16), v_ref[slot, block],
                        preferred_element_type=jnp.float32,
                    )
                buf[slot, peer, low : low + tile, :] = (total / denominator).astype(jnp.bfloat16)

        @pl.when(number > 0)
        def _():
            ship(number - 1)

        return carry

    lax.fori_loop(0, slots * ranks, one, 0)
    ship(slots * ranks - 1)
    for slot in range(slots):
        @pl.when(slot < mine)
        def _():
            pltpu.make_async_copy(
                buf.at[slot, me], columns(start + slot), local_sem.at[slot]
            ).wait()
            for hop in range(1, ranks):
                back(lax.rem(me + hop, ranks), slot).wait_send()

    for head in range(heads):
        owner, slot = head_owner(jnp.int32(head), ranks, heads, odd)

        @pl.when(owner != me)
        def _():
            pltpu.make_async_remote_copy(
                src_ref=buf.at[0, 0], dst_ref=columns(head), send_sem=send_sem.at[0, 0],
                recv_sem=recv_sem.at[head], device_id={"seq": owner}, device_id_type=MESH,
            ).wait_recv()


def attend(ranks, heads, queries, keys, values, valid):
    slots, _, local_img, hd = queries.shape
    vmem = pl.BlockSpec(memory_space=pltpu.VMEM)
    return pl.pallas_call(
        functools.partial(attend_kernel, ranks, heads),
        out_shape=jax.ShapeDtypeStruct((local_img, heads * hd), jnp.bfloat16),
        in_specs=[vmem] * 4,
        out_specs=pl.BlockSpec(memory_space=pl.ANY),
        scratch_shapes=[
            pltpu.VMEM((slots, ranks, local_img, hd), jnp.bfloat16),
            pltpu.SemaphoreType.DMA((slots, ranks)),
            pltpu.SemaphoreType.DMA((heads,)),
            pltpu.SemaphoreType.DMA((slots,)),
        ],
        compiler_params=pltpu.CompilerParams(
            collective_id=1, has_side_effects=True, vmem_limit_bytes=VMEM_LIMIT
        ),
    )(queries, keys, values, valid)


def reduce_kernel(
    size, att_ref, w_ref, out_ref, first, first_in, second, second_in, sems1, sems2
):
    me = lax.axis_index("tensor")
    core = lax.rem(me, 2)
    chip = me // 2
    chips = size // 2
    partner = 2 * chip + 1 - core
    rows = att_ref.shape[0] // size

    barrier = pltpu.get_barrier_semaphore()
    pl.semaphore_signal(barrier, inc=1, device_id={"tensor": partner}, device_id_type=MESH)
    for hop in range(1, chips):
        pl.semaphore_signal(
            barrier, inc=1, device_id={"tensor": 2 * lax.rem(chip + hop, chips) + core},
            device_id_type=MESH,
        )
    pl.semaphore_wait(barrier, chips)

    def partial(owner):
        block = att_ref[pl.ds(pl.multiple_of(owner * rows, rows), rows), :]
        return jnp.dot(block, w_ref[...], preferred_element_type=jnp.float32)

    def to_partner(hop):
        return pltpu.make_async_remote_copy(
            src_ref=first.at[hop], dst_ref=first_in.at[hop],
            send_sem=sems1.at[0, hop], recv_sem=sems1.at[1, hop],
            device_id={"tensor": partner}, device_id_type=MESH,
        )

    def to_chip(hop):
        return pltpu.make_async_remote_copy(
            src_ref=second.at[hop], dst_ref=second_in.at[hop],
            send_sem=sems2.at[0, hop], recv_sem=sems2.at[1, hop],
            device_id={"tensor": 2 * lax.rem(chip + hop, chips) + core}, device_id_type=MESH,
        )

    order = list(range(1, chips)) + [0]
    for hop in order:
        target = lax.rem(chip + hop, chips)
        first[hop] = partial(2 * target + 1 - core).astype(jnp.bfloat16)
        own = partial(2 * target + core)
        to_partner(hop).start()
        to_partner(hop).wait_recv()
        total = own + first_in[hop].astype(jnp.float32)
        if hop:
            second[hop] = total.astype(jnp.bfloat16)
            to_chip(hop).start()
        else:
            out_ref[...] = total
    for hop in range(1, chips):
        to_chip(hop).wait_recv()
        out_ref[...] += second_in[hop].astype(jnp.float32)
    for hop in range(chips):
        to_partner(hop).wait_send()
        if hop:
            to_chip(hop).wait_send()


def project_reduce(size, attended, image_out):
    tokens, width = attended.shape[0], image_out.shape[1]
    rows, chips = tokens // size, size // 2
    vmem = pl.BlockSpec(memory_space=pltpu.VMEM)
    stack = pltpu.VMEM((chips, rows, width), jnp.bfloat16)
    return pl.pallas_call(
        functools.partial(reduce_kernel, size),
        out_shape=jax.ShapeDtypeStruct((rows, width), jnp.float32),
        in_specs=[vmem] * 2,
        out_specs=vmem,
        scratch_shapes=[
            stack, stack, stack, stack,
            pltpu.SemaphoreType.DMA((2, chips)),
            pltpu.SemaphoreType.DMA((2, chips)),
        ],
        compiler_params=pltpu.CompilerParams(
            collective_id=2, has_side_effects=True, vmem_limit_bytes=VMEM_LIMIT
        ),
    )(attended, image_out)


def total_kernel(sizes, x_ref, out_ref, *scratch):
    me = {axis: lax.axis_index(axis) for axis, _ in sizes}
    barrier = pltpu.get_barrier_semaphore()
    count = 0
    for axis, size in sizes:
        for hop in range(1, size):
            pl.semaphore_signal(
                barrier, inc=1, device_id={axis: lax.rem(me[axis] + hop, size)},
                device_id_type=MESH,
            )
            count += 1
    pl.semaphore_wait(barrier, count)
    held = x_ref
    for number, (axis, size) in enumerate(sizes):
        slots, total, sems = scratch[3 * number : 3 * number + 3]
        copies = []
        for hop in range(1, size):
            copy = pltpu.make_async_remote_copy(
                src_ref=held, dst_ref=slots.at[hop], send_sem=sems.at[0, hop],
                recv_sem=sems.at[1, hop],
                device_id={axis: lax.rem(me[axis] + hop, size)}, device_id_type=MESH,
            )
            copy.start()
            copies.append(copy)
        sum_now = held[...]
        for hop, copy in enumerate(copies, 1):
            copy.wait()
            sum_now = sum_now + slots[hop]
        total[...] = sum_now
        held = total
    out_ref[...] = held[...]


def total_sum(sizes, tile):
    vmem = pl.BlockSpec(memory_space=pltpu.VMEM)
    scratch = []
    for _, size in sizes:
        scratch += [
            pltpu.VMEM((size,) + tile.shape, jnp.float32),
            pltpu.VMEM(tile.shape, jnp.float32),
            pltpu.SemaphoreType.DMA((2, size)),
        ]
    return pl.pallas_call(
        functools.partial(total_kernel, sizes),
        out_shape=jax.ShapeDtypeStruct(tile.shape, jnp.float32),
        in_specs=[vmem],
        out_specs=vmem,
        scratch_shapes=scratch,
        compiler_params=pltpu.CompilerParams(collective_id=3, has_side_effects=True),
    )(tile)


def gather_features(block, size):
    slot = lax.axis_index("tensor")
    chips = size // 2
    chip, core = slot // 2, lax.rem(slot, 2)
    held = [block]
    for hop in range(1, chips):
        held.append(
            lax.ppermute(
                block, "tensor",
                [(t, 2 * ((t // 2 + hop) % chips) + t % 2) for t in range(size)],
            )
        )
    other = [lax.ppermute(b, "tensor", [(t, t ^ 1) for t in range(size)]) for b in held]
    pairs = [
        jnp.where(core == 0, jnp.concatenate([a, b], axis=1), jnp.concatenate([b, a], axis=1))
        for a, b in zip(held, other)
    ]
    if chips == 2:
        return jnp.where(
            chip == 0,
            jnp.concatenate([pairs[0], pairs[1]], axis=1),
            jnp.concatenate([pairs[1], pairs[0]], axis=1),
        )
    stacked = jnp.stack(pairs)
    return jnp.concatenate([stacked[lax.rem(chip - c + chips, chips)] for c in range(chips)], axis=1)


def shards(
    image_states, text_states, image_qkv, text_qkv, image_out, final_weight, query_gain, key_gain,
    modulation, latent, old_velocity, rollout_noise, group_ids, text_lengths, step_ids,
):
    local_img = image_states.shape[1]
    local_txt = text_states.shape[1]
    hd = query_gain.shape[0]
    heads = image_qkv.shape[2] // hd
    total_steps = modulation.shape[0]
    ranks = lax.axis_size("seq")
    size = lax.axis_size("tensor")
    row_count = local_img // size
    slot = lax.axis_index("tensor")
    group = group_ids[0]
    modrows = modulation[step_ids[0]]
    length = text_lengths[group]
    joined = jnp.concatenate([text_states[group], image_states[0]], axis=0)
    full = gather_features(joined, size)
    wimg = jnp.transpose(image_qkv, (1, 0, 2))
    wtxt = jnp.transpose(text_qkv[:, 1:, :], (1, 0, 2))
    text_f = full[:local_txt].astype(jnp.float32)
    image_f = full[local_txt:].astype(jnp.float32)
    normed_img = (layer_norm(image_f) * (1.0 + modrows[1]) + modrows[0]).astype(jnp.bfloat16)
    normed_txt = (layer_norm(text_f) * (1.0 + modrows[4]) + modrows[3]).astype(jnp.bfloat16)
    queries, keys, values = project(
        ranks, heads, normed_img, normed_txt, wimg, wtxt, query_gain, key_gain
    )
    place = jnp.arange(local_txt + local_img, dtype=jnp.int32)[None, :]
    text_pos = jnp.arange(ranks, dtype=jnp.int32)[:, None] * local_txt + place
    valid = ((place >= local_txt) | (text_pos < length)).astype(jnp.float32)[:, None, :]
    attended = attend(ranks, heads, queries, keys, values, valid)
    summed = project_reduce(size, attended, image_out)
    own_rows = lax.dynamic_slice_in_dim(
        full, local_txt + slot * row_count, row_count, 0
    ).astype(jnp.float32)
    resid = own_rows + modrows[2] * summed
    final_normed = (layer_norm(resid) * (1.0 + modrows[6]) + modrows[5]).astype(jnp.bfloat16)
    velocity = jnp.dot(final_normed, final_weight, preferred_element_type=jnp.float32)[None]
    flow_time, step_delta, noise_sigma, spread = plan(step_ids, total_steps)
    flow_e = flow_time[:, None, None]
    sigma_e = noise_sigma[:, None, None]
    step_mean = drift_mean(latent, velocity, flow_e, step_delta, sigma_e)
    mean_old = drift_mean(latent, old_velocity.astype(jnp.float32), flow_e, step_delta, sigma_e)
    shifted = rollout_noise + (mean_old - step_mean) / spread[:, None, None]
    partial_ratio = jnp.sum(rollout_noise * rollout_noise - shifted * shifted) * 0.5
    tile = jnp.broadcast_to(partial_ratio, (8, 128))
    ratio_total = total_sum((("tensor", size), ("seq", ranks)), tile)[0, :1]
    elements = latent.shape[1] * ranks * size * latent.shape[2]
    return (step_mean, ratio_total / elements)


def solution(mesh):
    placed = (
        P("dp", "seq", "tensor"),
        P(None, "seq", "tensor"),
        P(None, None, "tensor"),
        P(None, None, "tensor"),
        P("tensor", None),
        P(),
        P(),
        P(),
        P(),
        P("dp", ("seq", "tensor"), None),
        P("dp", ("seq", "tensor"), None),
        P("dp", ("seq", "tensor"), None),
        P("dp"),
        P(),
        P("dp"),
    )
    return jax.shard_map(
        shards,
        mesh=mesh,
        in_specs=placed,
        out_specs=(P("dp", ("seq", "tensor"), None), P("dp")),
        check_vma=False,
    )
```

time: 345 us -> 179 us (0.52)
  Pallas kernels: 0 us -> 130 us
  waiting for transfers between devices: 126 us -> 10.4 us
  local copies, waits for them, and re-layouts: 66.6 us -> 10.6 us
  matrix products: 57.8 us -> 1.84 us
  blocking collectives: 54.5 us -> 0 us
  between operations: 18.5 us -> 4.78 us
    pallas_call x0 -> x4, Pallas kernels: none -> 130 us  [the longest x1 64.4 us: project(): pl.pallas_call(functools.partial(project_kernel, ranks, heads, group), gr...]
    all_gather x3 -> x0, waiting for transfers between devices: 92.2 us -> none  [the longest x1 48.5 us: shards(): lax.all_gather(value_rows, 'seq', axis=1, tiled=True)]
    dot_general x8 -> x1, matrix products: 57.8 us -> 1.84 us  [shards(): jnp.dot(final_normed, final_weight, preferred_element_type=jnp.float32)]
    unnamed x46 -> x16, local copies, waits for them, and re-layouts: 42.4 us -> 0.35 us
    psum x1 -> x0, blocking collectives: 33.2 us -> none  [shards(): ratio_total = lax.psum(partial_ratio, ('seq', 'tensor'))]
    reduce_scatter x1 -> x0, waiting for transfers between devices: 33 us -> none  [shards(): lax.psum_scatter(jnp.einsum('tsk,kd->tsd', attended, image_out, preferred...]
    unnamed x1 -> x0, blocking collectives: 13.2 us -> none
    all_gather x2 -> x0, local copies, waits for them, and re-layouts: 11.6 us -> none  [the longest x1 5.82 us: shards(): lax.all_gather(value_rows, 'seq', axis=1, tiled=True)]
  transfers between devices with their start and end apart: 4 -> 3, of which waited for: 3 -> 1; matrix products, arithmetic and copies ran while one was open for 26% -> 8% of each run, Pallas kernels for 0% -> 0%
where the time goes in v1:
time: 179 us
  Pallas kernels  130 us (73%)
  other arithmetic  18.3 us (10%)
  local copies, waits for them, and re-layouts  10.6 us (6%)
  waiting for transfers between devices  10.4 us (6%)
  between operations  4.78 us (3%)
  starting transfers between devices  3.07 us (2%)
  matrix products  1.84 us (1%)
    pallas_call x1, Pallas kernels, project(): pl.pallas_call(functools.partial(project_kernel, ranks, heads, group), gr...  64.4 us
    pallas_call x1, Pallas kernels, project_reduce(): pl.pallas_call(functools.partial(reduce_kernel, size), out_shape=jax.Shap...  31 us
    pallas_call x1, Pallas kernels, attend(): pl.pallas_call(functools.partial(attend_kernel, ranks, heads), out_shape=...  24.9 us
    ppermute x1, waiting for transfers between devices, gather_features(): lax.ppermute(block, 'tensor', [(t, 2 * ((t // 2 + hop) % chips) + t % 2)...  10.3 us
    pallas_call x1, Pallas kernels, total_sum(): pl.pallas_call(functools.partial(total_kernel, sizes), out_shape=jax.Shap...  9.43 us
    transpose x1, local copies, waits for them, and re-layouts, shards(): wtxt = jnp.transpose(text_qkv[:, 1:, :], (1, 0, 2))  7.91 us
  transfers between devices with their start and end apart: 3, of which 1 were waited for; matrix products, arithmetic and copies ran while one was open for 8% of the time, Pallas kernels for 0%

profile of v1, /device:TPU:0, one launch (start us, length us, event | category | flops | bytes accessed | tf_op | source)
XLA Modules:
  0.0 178.7 jit_solution(6278785160142663438)
XLA Ops:
  1.3 0.3 copy-done
  1.7 1.2 pad_maximum_fusion
  2.9 3.1 %collective-permute-start.1 = (bf16[576,768]{1,0:T(8,128)(2,1)S(1)}, bf16[576,768]{1,0:T(8,128)(2,1)S(1)}, u32[]{:S(2)}, u32[]{:S(2)}) collective-permute-start(bf16[576,768]{1,0:T(8,128)(2,1)S(1)} %pad_maximum_fusion), channel_id=1, source_target_pairs={{0,2},{1,3},{2,0},{3,1},{4,6},{5,7},{6,4},{7,5},{8,10},{9,11},{10,... | collective-permute-start | bytes 2654216 | tf_op jit(solution)/shard_map/ppermute | solution.py:475
  5.9 7.9 %slice_bitcast_fusion.wtxt_ref = bf16[2,3072,768]{2,1,0:T(8,128)(2,1)} fusion(bf16[3072,3,768]{2,0,1:T(8,128)(2,1)} %param.18), kind=kLoop, calls=%fused_computation | loop fusion | bytes 18874368 | tf_op jit(solution)/shard_map/transpose | solution.py:514
  14.5 0.6 dynamic_slice.15
  15.2 10.3 %collective-permute-done.1 = bf16[576,768]{1,0:T(8,128)(2,1)S(1)} collective-permute-done((bf16[576,768]{1,0:T(8,128)(2,1)S(1)}, bf16[576,768]{1,0:T(8,128)(2,1)S(1)}, u32[]{:S(2)}, u32[]{:S(2)}) %collective-permute-start.1) | collective-permute-done | bytes 884768 | tf_op jit(solution)/shard_map/ppermute | solution.py:475
  25.6 1.2 or_convert_fusion.valid_ref
  26.8 1.5 constant_dynamic-slice_fusion.2
  28.3 2.9 %maximum_select_fusion.1 = bf16[576,1536]{1,0:T(8,128)(2,1)S(1)} fusion(bf16[576,768]{1,0:T(8,128)(2,1)} %collective-permute-done, bf16[512,768]{1,0:T(8,128)(2,1)S(1)} %bitcast.43, bf16[64,768]{1,0:T(8,128)(2,1)S(1)} %dynamic-slice_bitcast_fusion, pred[]{:T(512)S(6)} %eq.8), kind=kLoop, calls=%fused_computation.10 | loop fusion | flops 11501568 | bytes 3538945 | tf_op jit(solution)/shard_map/jit(_where)/select_n | solution.py:482
  31.2 0.5 maximum_select_fusion.2
  31.7 1.0 maximum_select_fusion
  32.9 0.5 convert_reduce_fusion
  33.7 1.0 fusion.2
  34.6 1.0 fusion.11.txt_ref
  35.6 3.4 %fusion.5.img_ref = bf16[512,3072]{1,0:T(8,128)(2,1)} fusion(f32[3072]{0:T(1024)S(1)} %bitcast.49, f32[3072]{0:T(1024)S(1)} %bitcast.50, f32[512]{0:T(512)S(1)} %add_rsqrt_fusion, f32[512]{0:T(512)S(1)} %broadcast_multiply_fusion, bf16[576,3072]{1,0:T(8,128)(2,1)S(1)} %maximum_select_fusion), kind=kLoop, calls=%fused_computation.8 | loop fusion | flops 9437184 | bytes 6320128 | tf_op jit(solution)/shard_map/convert_element_type | solution.py:517
  39.0 64.4 %shard_map.158 = (bf16[2,4,512,128]{3,2,1,0:T(8,128)(2,1)}, bf16[2,4,576,128]{3,2,1,0:T(8,128)(2,1)}, bf16[2,4,576,128]{3,2,1,0:T(8,128)(2,1)}) custom-call(bf16[512,3072]{1,0:T(8,128)(2,1)} %fusion.5.img_ref, bf16[64,3072]{1,0:T(8,128)(2,1)} %fusion.11.txt_ref, bf16[3,3072,768]{2,1,0:T(8,128)(2,1)} %bitcast.41, ...), custom_call_target="tpu_custom_call" | custom-call | tf_op jit(solution)/shard_map/pallas_call | solution.py:192
  103.5 24.9 %shard_map.159.att_ref = bf16[512,768]{1,0:T(8,128)(2,1)} custom-call(bf16[2,4,512,128]{3,2,1,0:T(8,128)(2,1)} %get-tuple-element.5.q_ref, bf16[2,4,576,128]{3,2,1,0:T(8,128)(2,1)} %get-tuple-element.6.k_ref, bf16[2,4,576,128]{3,2,1,0:T(8,128)(2,1)} %get-tuple-element.7.v_ref, f32[4,1,576]{2,1,0:T(1,128)} %or_convert_fusion.valid_ref), custom_call_target="tpu_custom_call" | custom-call | tf_op jit(solution)/shard_map/pallas_call | solution.py:319
  128.4 31.0 %shard_map.160 = f32[128,3072]{1,0:T(8,128)} custom-call(bf16[512,768]{1,0:T(8,128)(2,1)} %shard_map.159.att_ref, bf16[768,3072]{1,0:T(8,128)(2,1)} %w_ref.1), custom_call_target="tpu_custom_call" | custom-call | tf_op jit(solution)/shard_map/pallas_call | solution.py:400
  159.5 1.9 %fusion.13 = f32[128]{0:T(128)S(1)} fusion(f32[128,3072]{1,0:T(8,128)} %shard_map.160, f32[3072]{0:T(1024)S(1)} %bitcast.44, bf16[576,3072]{1,0:T(8,128)(2,1)S(1)} %maximum_select_fusion, s32[]{:T(128)S(6)} %select_n.42), kind=kLoop, calls=%fused_computation.25 | loop fusion | flops 1572736 | bytes 2372100 | tf_op jit(solution)/shard_map/reduce_sum | solution.py:16
  161.3 1.8 %multiply_reduce_fusion = f32[128]{0:T(128)S(1)} fusion(f32[128]{0:T(128)S(1)} %broadcast_multiply_fusion.1, f32[128,3072]{1,0:T(8,128)} %shard_map.160, f32[3072]{0:T(1024)S(1)} %bitcast.45, bf16[576,3072]{1,0:T(8,128)(2,1)S(1)} %maximum_select_fusion, s32[]{:T(128)S(6)} %select_n.42), kind=kLoop, calls=%fused_computation.13 | loop fusion | flops 2359168 | bytes 2372612 | tf_op jit(solution)/shard_map/reduce_sum | solution.py:18
  163.2 1.8 %fusion.27 = (f32[]{:T(128)}, f32[1,128,64]{1,2,0:T(8,128)}) fusion(f32[1,128,64]{1,2,0:T(8,128)S(1)} %copy-done.4, f32[1,128,64]{1,2,0:T(8,128)S(1)} %copy-done.5, bf16[1,128,64]{1,2,0:T(8,128)(2,1)S(1)} %copy-done.6, f32[]{:T(128)} %bitcast.20, f32[]{:T(128)} %bitcast.18, f32[]{:T(128)} %bitcast.17, bf16[3072,64]{0,1:T(8,128)(2,1)S(1)} %copy-done.3, ...), kind=kOutput, calls=%fused_computation.44 | convolution fusion | flops 53641216 | bytes 2907144 | tf_op jit(solution)/shard_map/dot_general | solution.py:532
  165.7 0.6 broadcast_in_dim.11.x_ref
  166.3 9.4 %shard_map.161 = f32[8,128]{1,0:T(8,128)} custom-call(f32[8,128]{1,0:T(8,128)} %broadcast_in_dim.11.x_ref), custom_call_target="tpu_custom_call" | custom-call | tf_op jit(solution)/shard_map/pallas_call | solution.py:458
  175.7 1.2 slice.50
  (30 shorter events, 0.5 us)
Async XLA Ops:
  0.6 1.0 copy-start
  2.8 11.7 %copy-start.7 = (s32[4]{0:T(128)S(1)}, s32[4]{0:T(128)}, u32[]{:S(2)}) copy-start(s32[4]{0:T(128)} %param.28) | copy-start | bytes 52
  2.9 25.4 %copy-start.2 = (bf16[1,512,768]{2,1,0:T(8,128)(2,1)S(1)}, bf16[1,512,768]{2,1,0:T(8,128)(2,1)}, u32[]{:S(2)}) copy-start(bf16[1,512,768]{2,1,0:T(8,128)(2,1)} %param.15) | copy-start | bytes 2359300
  2.9 22.7 %collective-permute-start.1 = (bf16[576,768]{1,0:T(8,128)(2,1)S(1)}, bf16[576,768]{1,0:T(8,128)(2,1)S(1)}, u32[]{:S(2)}, u32[]{:S(2)}) collective-permute-start(bf16[576,768]{1,0:T(8,128)(2,1)S(1)} %pad_maximum_fusion), channel_id=1, source_target_pairs={{0,2},{1,3},{2,0},{3,1},{4,6},{5,7},{6,4},{7,5},{8,10},{9,11},{10,... | collective-permute-start | bytes 2654216 | tf_op jit(solution)/shard_map/ppermute | solution.py:475
  5.9 22.4 %collective-permute-start = (bf16[576,768]{1,0:T(8,128)(2,1)S(1)}, bf16[576,768]{1,0:T(8,128)(2,1)}, u32[]{:S(2)}, u32[]{:S(2)}) collective-permute-start(bf16[576,768]{1,0:T(8,128)(2,1)S(1)} %pad_maximum_fusion), channel_id=1, source_target_pairs={{0,1},{1,0},{2,3},{3,2},{4,5},{5,4},{6,7},{7,6},{8,9},{9,8},{10,11... | collective-permute-start | bytes 2654216 | tf_op jit(solution)/shard_map/ppermute | solution.py:480
  25.6 5.6 %collective-permute-start.2 = (bf16[576,768]{1,0:T(8,128)(2,1)S(1)}, bf16[576,768]{1,0:T(8,128)(2,1)S(1)}, u32[]{:S(2)}, u32[]{:S(2)}) collective-permute-start(bf16[576,768]{1,0:T(8,128)(2,1)S(1)} %collective-permute-done.1), channel_id=1, source_target_pairs={{0,1},{1,0},{2,3},{3,2},{4,5},{5,4},{6,7},{7,6},{8,9},{9,8},{10,11... | collective-permute-start | bytes 2654216 | tf_op jit(solution)/shard_map/ppermute | solution.py:480
  159.4 3.8 %copy-start.1 = (f32[128,3072]{1,0:T(8,128)S(1)}, f32[128,3072]{1,0:T(8,128)}, u32[]{:S(2)}) copy-start(f32[128,3072]{1,0:T(8,128)} %shard_map.160) | copy-start | bytes 4718596
  159.4 3.8 %copy-start.3 = (bf16[3072,64]{0,1:T(8,128)(2,1)S(1)}, bf16[3072,64]{0,1:T(8,128)(2,1)}, u32[]{:S(2)}) copy-start(bf16[3072,64]{0,1:T(8,128)(2,1)} %param.20) | copy-start | bytes 1179652
  159.4 3.8 %copy-start.4 = (f32[1,128,64]{1,2,0:T(8,128)S(1)}, f32[1,128,64]{1,2,0:T(8,128)}, u32[]{:S(2)}) copy-start(f32[1,128,64]{1,2,0:T(8,128)} %param.26) | copy-start | bytes 98308
  159.4 3.8 %copy-start.5 = (f32[1,128,64]{1,2,0:T(8,128)S(1)}, f32[1,128,64]{1,2,0:T(8,128)}, u32[]{:S(2)}) copy-start(f32[1,128,64]{1,2,0:T(8,128)} %param.24) | copy-start | bytes 98308
  159.4 3.8 %copy-start.6 = (bf16[1,128,64]{1,2,0:T(8,128)(2,1)S(1)}, bf16[1,128,64]{1,2,0:T(8,128)(2,1)}, u32[]{:S(2)}) copy-start(bf16[1,128,64]{1,2,0:T(8,128)(2,1)} %param.25) | copy-start | bytes 49156

commit v2 on v1

--- a/solution.py
+++ b/solution.py
@@ -69,166 +69,239 @@
 
 
 def project_kernel(
-    ranks, heads, group, img_ref, txt_ref, wimg_ref, wtxt_ref, qgain_ref, kgain_ref,
-    q_out, k_out, v_out, qbuf, kvbuf, send_sem, recv_sem, local_sem,
+    ranks, size, heads, local_txt, chunk, x_ref, mod_ref, wimg_hbm, wtxt_hbm, qgain_ref, kgain_ref,
+    out, own_ref, gathered, normed, staged, wimg, wtxt,
+    wsem, chip_send, chip_recv, core_send, core_recv, pass_send, pass_recv, own_sem,
+    send_sem, recv_sem, local_sem,
 ):
     me = lax.axis_index("seq")
-    odd = lax.rem(lax.axis_index("tensor"), 2)
-    step = pl.program_id(0)
-    pieces = heads // group
-    steps = 3 * pieces
-    local_txt = txt_ref.shape[0]
-    slots = q_out.shape[0]
+    slot_t = lax.axis_index("tensor")
+    core, chip = lax.rem(slot_t, 2), slot_t // 2
+    chips = size // 2
+    partner = 2 * chip + 1 - core
+    rows, part = x_ref.shape
+    width = size * part
     hd = qgain_ref.shape[1]
-    dot = functools.partial(jnp.dot, preferred_element_type=jnp.float32)
-
-    @pl.when(step == 0)
-    def _():
-        meet("seq", ranks, me)
-
-    def normed(values, gain_ref):
+    slots = out.shape[0]
+    chunks = 1 + (rows - local_txt) // chunk
+
+    def span(number):
+        if number == 0:
+            return pl.ds(0, local_txt)
+        return pl.ds(local_txt + (number - 1) * chunk, chunk)
+
+    def at_chip(hop):
+        return 2 * lax.rem(chip + hop + chips, chips) + core
+
+    weight_copies = (
+        pltpu.make_async_copy(wtxt_hbm.at[pl.ds(1, 2)], wtxt, wsem.at[0]),
+        pltpu.make_async_copy(wimg_hbm, wimg, wsem.at[1]),
+    )
+    for copy in weight_copies:
+        copy.start()
+    own_copy = pltpu.make_async_copy(x_ref, gathered.at[slot_t], own_sem)
+    own_copy.start()
+
+    barrier = pltpu.get_barrier_semaphore()
+    for hop in range(1, ranks):
+        pl.semaphore_signal(
+            barrier, inc=1, device_id={"seq": lax.rem(me + hop, ranks)}, device_id_type=MESH
+        )
+    pl.semaphore_signal(barrier, inc=1, device_id={"tensor": partner}, device_id_type=MESH)
+    for hop in range(1, chips):
+        pl.semaphore_signal(barrier, inc=1, device_id={"tensor": at_chip(hop)}, device_id_type=MESH)
+    pl.semaphore_wait(barrier, ranks - 1 + chips)
+
+    def chip_copy(number, hop):
+        return pltpu.make_async_remote_copy(
+            src_ref=x_ref.at[span(number)], dst_ref=gathered.at[slot_t, span(number)],
+            send_sem=chip_send.at[number, hop], recv_sem=chip_recv.at[number, hop],
+            device_id={"tensor": at_chip(hop)}, device_id_type=MESH,
+        )
+
+    def core_copy(number):
+        return pltpu.make_async_remote_copy(
+            src_ref=x_ref.at[span(number)], dst_ref=gathered.at[slot_t, span(number)],
+            send_sem=core_send.at[number], recv_sem=core_recv.at[number],
+            device_id={"tensor": partner}, device_id_type=MESH,
+        )
+
+    def pass_copy(number, hop):
+        block = gathered.at[at_chip(-hop), span(number)]
+        return pltpu.make_async_remote_copy(
+            src_ref=block, dst_ref=block,
+            send_sem=pass_send.at[number, hop], recv_sem=pass_recv.at[number, hop],
+            device_id={"tensor": partner}, device_id_type=MESH,
+        )
+
+    for number in range(chunks):
+        for hop in range(1, chips):
+            chip_copy(number, hop).start()
+        core_copy(number).start()
+    own_copy.wait()
+
+    def arrive(number):
+        for hop in range(1, chips):
+            chip_copy(number, hop).wait_recv()
+            pass_copy(number, hop).start()
+
+    def head_scale(values, gain_ref):
         mean_square = jnp.mean(values * values, axis=-1, keepdims=True)
         return (values * lax.rsqrt(mean_square + NORM_EPSILON) * gain_ref[...]).astype(jnp.bfloat16)
 
-    piece = lax.rem(step, pieces)
-    kind = step // pieces
-    img = dot(img_ref[...], wimg_ref[0])
-
-    @pl.when(kind < 2)
-    def _():
-        txt = dot(txt_ref[...], wtxt_ref[0])
-        for g in range(group):
-            cols = slice(g * hd, (g + 1) * hd)
-            head = kind * heads + piece * group + g
-
-            @pl.when(kind == 0)
+    def head_copy(number, head, slot, owner):
+        cols = pl.ds(0, 2 * hd if number == 0 else 3 * hd)
+        return pltpu.make_async_remote_copy(
+            src_ref=staged.at[head, span(number), cols],
+            dst_ref=out.at[slot, me, span(number), cols],
+            send_sem=send_sem.at[number, head],
+            recv_sem=recv_sem.at[number, slot, me],
+            device_id={"seq": owner}, device_id_type=MESH,
+        )
+
+    def local_copy(number, head, slot):
+        cols = pl.ds(0, 2 * hd if number == 0 else 3 * hd)
+        return pltpu.make_async_copy(
+            staged.at[head, span(number), cols], out.at[slot, me, span(number), cols],
+            local_sem.at[number, slot],
+        )
+
+    odd = core
+    arrive(0)
+    for number in range(chunks):
+        here = span(number)
+        count = here.size
+        core_copy(number).wait_recv()
+        for hop in range(1, chips):
+            pass_copy(number, hop).wait_recv()
+        if number + 1 < chunks and number > 0:
+            arrive(number + 1)
+        shift, gain = (3, 4) if number == 0 else (0, 1)
+        pieces = [gathered[t, here, :].astype(jnp.float32) for t in range(size)]
+        total = sum(jnp.sum(p, axis=-1, keepdims=True) for p in pieces)
+        mean = total / width
+        square = sum(jnp.sum((p - mean) * (p - mean), axis=-1, keepdims=True) for p in pieces)
+        scale = lax.rsqrt(square / width + NORM_EPSILON)
+        for t in range(size):
+            cols = slice(t * part, (t + 1) * part)
+            p = gathered[t, here, :].astype(jnp.float32)
+            normed[:count, cols] = (
+                (p - mean) * scale * (1.0 + mod_ref[gain : gain + 1, cols])
+                + mod_ref[shift : shift + 1, cols]
+            ).astype(jnp.bfloat16)
+        if number < 2:
+            weight_copies[number].wait()
+        for kind in range(2 if number == 0 else 3):
+            weight = wtxt.at[kind] if number == 0 else wimg.at[(kind + 1) % 3]
+            product = jnp.dot(normed[:count, :], weight[...], preferred_element_type=jnp.float32)
+            for head in range(heads):
+                values = product[:, head * hd : (head + 1) * hd]
+                if kind == 1:
+                    values = values.astype(jnp.bfloat16)
+                else:
+                    values = head_scale(values, kgain_ref if kind == 0 else qgain_ref)
+                staged[head, here, kind * hd : (kind + 1) * hd] = values
+        for head in range(heads):
+            owner, slot = head_owner(jnp.int32(head), ranks, heads, odd)
+
+            @pl.when(owner == me)
             def _():
-                kvbuf[head, :local_txt, :] = normed(txt[:, cols], kgain_ref)
-                kvbuf[head, local_txt:, :] = normed(img[:, cols], kgain_ref)
-
-            @pl.when(kind == 1)
+                local_copy(number, head, slot).start()
+
+            @pl.when(owner != me)
             def _():
-                kvbuf[head, :local_txt, :] = txt[:, cols].astype(jnp.bfloat16)
-                kvbuf[head, local_txt:, :] = img[:, cols].astype(jnp.bfloat16)
-
-    @pl.when(kind == 2)
-    def _():
-        for g in range(group):
-            qbuf[piece * group + g] = normed(img[:, g * hd : (g + 1) * hd], qgain_ref)
-
-    def ship(which):
-        kind_of = which // pieces
-        for g in range(group):
-            head = lax.rem(which, pieces) * group + g
-            owner, slot = head_owner(head, ranks, heads, odd)
-            for number, out in ((0, k_out), (1, v_out), (2, q_out)):
-                source = qbuf.at[head] if number == 2 else kvbuf.at[number * heads + head]
-
-                @pl.when((kind_of == number) & (owner == me))
-                def _():
-                    pltpu.make_async_copy(
-                        source, out.at[slot, me], local_sem.at[number, slot]
-                    ).start()
-
-                @pl.when((kind_of == number) & (owner != me))
-                def _():
+                head_copy(number, head, slot, owner).start()
+
+        if number == 0:
+            arrive(1)
+
+    for t in range(size):
+        mine_rows = own_ref.shape[0]
+        own_ref[:, t * part : (t + 1) * part] = gathered[
+            t, pl.ds(local_txt + slot_t * mine_rows, mine_rows), :
+        ]
+
+    mine = first_head(me + 1, ranks, heads, odd) - first_head(me, ranks, heads, odd)
+    for number in range(chunks):
+        core_copy(number).wait_send()
+        for hop in range(1, chips):
+            chip_copy(number, hop).wait_send()
+            pass_copy(number, hop).wait_send()
+        for head in range(heads):
+            owner, slot = head_owner(jnp.int32(head), ranks, heads, odd)
+
+            @pl.when(owner != me)
+            def _():
+                head_copy(number, head, slot, owner).wait_send()
+
+        for slot in range(slots):
+            @pl.when(slot < mine)
+            def _():
+                local_copy(number, 0, slot).wait()
+                for hop in range(1, ranks):
+                    peer = lax.rem(me + hop, ranks)
+                    cols = pl.ds(0, 2 * hd if number == 0 else 3 * hd)
                     pltpu.make_async_remote_copy(
-                        src_ref=source,
-                        dst_ref=out.at[slot, me],
-                        send_sem=send_sem.at[number, head],
-                        recv_sem=recv_sem.at[number, slot, me],
-                        device_id={"seq": owner},
-                        device_id_type=MESH,
-                    ).start()
-
-    @pl.when(step > 0)
-    def _():
-        ship(step - 1)
-
-    @pl.when(step == steps - 1)
-    def _():
-        ship(step)
-        mine = first_head(me + 1, ranks, heads, odd) - first_head(me, ranks, heads, odd)
-        for number, out in ((0, k_out), (1, v_out), (2, q_out)):
-            buf = qbuf if number == 2 else kvbuf
-
-            for head in range(heads):
-                owner, _ = head_owner(jnp.int32(head), ranks, heads, odd)
-
-                @pl.when(owner != me)
-                def _():
-                    src = buf.at[head]
-                    pltpu.make_async_remote_copy(
-                        src_ref=src, dst_ref=out.at[0, me],
-                        send_sem=send_sem.at[number, head], recv_sem=recv_sem.at[number, 0, me],
-                        device_id={"seq": owner}, device_id_type=MESH,
-                    ).wait_send()
-
-            for slot in range(slots):
-                @pl.when(slot < mine)
-                def _():
-                    pltpu.make_async_copy(
-                        buf.at[0], out.at[slot, me], local_sem.at[number, slot]
-                    ).wait()
-                    for hop in range(1, ranks):
-                        peer = lax.rem(me + hop, ranks)
-                        pltpu.make_async_remote_copy(
-                            src_ref=buf.at[0], dst_ref=out.at[slot, peer],
-                            send_sem=send_sem.at[number, 0], recv_sem=recv_sem.at[number, slot, peer],
-                            device_id={"seq": peer}, device_id_type=MESH,
-                        ).wait_recv()
-
-
-def project(ranks, heads, normed_img, normed_txt, wimg, wtxt, query_gain, key_gain):
-    width = normed_img.shape[1]
+                        src_ref=staged.at[0, span(number), cols],
+                        dst_ref=out.at[slot, peer, span(number), cols],
+                        send_sem=send_sem.at[number, 0],
+                        recv_sem=recv_sem.at[number, slot, peer],
+                        device_id={"seq": peer}, device_id_type=MESH,
+                    ).wait_recv()
+
+
+def project(ranks, size, heads, local_txt, joined, modrows, wimg, wtxt, query_gain, key_gain):
     hd = query_gain.shape[0]
-    group = 2 if heads % 2 == 0 else 1
-    pieces = heads // group
+    rows, part = joined.shape
+    width = size * part
     slots = -(-heads // ranks)
-    local_img, local_txt = normed_img.shape[0], normed_txt.shape[0]
-    rows = local_img + local_txt
-    kv = jax.ShapeDtypeStruct((slots, ranks, rows, hd), jnp.bfloat16)
-    whole = pl.BlockSpec(memory_space=pltpu.VMEM)
+    local_img = rows - local_txt
+    chunk = 128 if local_img % 128 == 0 else local_img
+    chunks = 1 + local_img // chunk
+    chips = size // 2
+    vmem = pl.BlockSpec(memory_space=pltpu.VMEM)
+    anywhere = pl.BlockSpec(memory_space=pl.ANY)
+    dma = pltpu.SemaphoreType.DMA
     return pl.pallas_call(
-        functools.partial(project_kernel, ranks, heads, group),
-        grid=(3 * pieces,),
-        out_shape=(jax.ShapeDtypeStruct((slots, ranks, local_img, hd), jnp.bfloat16), kv, kv),
-        in_specs=[
-            whole,
-            whole,
-            pl.BlockSpec((1, width, group * hd), lambda i: ((i // pieces + 1) % 3, 0, i % pieces)),
-            pl.BlockSpec(
-                (1, width, group * hd),
-                lambda i: (
-                    jnp.minimum(i // pieces, 1), 0,
-                    jnp.where(i < 2 * pieces, i % pieces, pieces - 1),
-                ),
-            ),
-            whole,
-            whole,
-        ],
-        out_specs=[pl.BlockSpec(memory_space=pl.ANY)] * 3,
+        functools.partial(project_kernel, ranks, size, heads, local_txt, chunk),
+        out_shape=(
+            jax.ShapeDtypeStruct((slots, ranks, rows, 3 * hd), jnp.bfloat16),
+            jax.ShapeDtypeStruct((local_img // size, width), jnp.bfloat16),
+        ),
+        in_specs=[vmem, vmem, anywhere, anywhere, vmem, vmem],
+        out_specs=(anywhere, vmem),
         scratch_shapes=[
-            pltpu.VMEM((heads, local_img, hd), jnp.bfloat16),
-            pltpu.VMEM((2 * heads, rows, hd), jnp.bfloat16),
-            pltpu.SemaphoreType.DMA((3, heads)),
-            pltpu.SemaphoreType.DMA((3, slots, ranks)),
-            pltpu.SemaphoreType.DMA((3, slots)),
+            pltpu.VMEM((size, rows, part), jnp.bfloat16),
+            pltpu.VMEM((max(chunk, local_txt), width), jnp.bfloat16),
+            pltpu.VMEM((heads, rows, 3 * hd), jnp.bfloat16),
+            pltpu.VMEM(wimg.shape, jnp.bfloat16),
+            pltpu.VMEM((2,) + wtxt.shape[1:], jnp.bfloat16),
+            dma((2,)),
+            dma((chunks, chips)),
+            dma((chunks, chips)),
+            dma((chunks,)),
+            dma((chunks,)),
+            dma((chunks, chips)),
+            dma((chunks, chips)),
+            dma,
+            dma((chunks, heads)),
+            dma((chunks, slots, ranks)),
+            dma((chunks, slots)),
         ],
         compiler_params=pltpu.CompilerParams(
-            collective_id=0, has_side_effects=True, vmem_limit_bytes=VMEM_LIMIT,
-            dimension_semantics=("arbitrary",),
+            collective_id=0, has_side_effects=True, vmem_limit_bytes=VMEM_LIMIT
         ),
-    )(normed_img, normed_txt, wimg, wtxt, query_gain[None, :], key_gain[None, :])
+    )(joined, modrows, wimg, wtxt, query_gain[None, :], key_gain[None, :])
 
 
 def attend_kernel(
-    ranks, heads, q_ref, k_ref, v_ref, valid_ref, out_ref, buf, send_sem, recv_sem, local_sem
+    ranks, heads, qkv_ref, valid_ref, out_ref, buf, send_sem, recv_sem, local_sem
 ):
     me = lax.axis_index("seq")
     odd = lax.rem(lax.axis_index("tensor"), 2)
     meet("seq", ranks, me)
-    slots, _, local_img, hd = q_ref.shape
+    slots, _, local_img, hd = buf.shape
+    local_txt = qkv_ref.shape[2] - local_img
     start = first_head(me, ranks, heads, odd)
     mine = first_head(me + 1, ranks, heads, odd) - start
     scale = math.log2(math.e) / math.sqrt(hd)
@@ -269,18 +342,18 @@
         @pl.when(slot < mine)
         def _():
             for low in range(0, local_img, tile):
-                queries = q_ref[slot, peer, low : low + tile, :]
+                queries = qkv_ref[slot, peer, local_txt + low : local_txt + low + tile, 2 * hd :]
                 total = jnp.zeros((tile, hd), jnp.float32)
                 denominator = jnp.zeros((tile, 1), jnp.float32)
                 for block in range(ranks):
                     scores = lax.dot_general(
-                        queries, k_ref[slot, block], (((1,), (1,)), ((), ())),
+                        queries, qkv_ref[slot, block, :, :hd], (((1,), (1,)), ((), ())),
                         preferred_element_type=jnp.float32,
                     )
                     weights = jnp.exp2(scores * scale) * valid_ref[block]
                     denominator = denominator + jnp.sum(weights, axis=-1, keepdims=True)
                     total = total + jnp.dot(
-                        weights.astype(jnp.bfloat16), v_ref[slot, block],
+                        weights.astype(jnp.bfloat16), qkv_ref[slot, block, :, hd : 2 * hd],
                         preferred_element_type=jnp.float32,
                     )
                 buf[slot, peer, low : low + tile, :] = (total / denominator).astype(jnp.bfloat16)
@@ -313,13 +386,13 @@
             ).wait_recv()
 
 
-def attend(ranks, heads, queries, keys, values, valid):
-    slots, _, local_img, hd = queries.shape
+def attend(ranks, heads, local_img, qkv, valid):
+    slots, hd = qkv.shape[0], qkv.shape[3] // 3
     vmem = pl.BlockSpec(memory_space=pltpu.VMEM)
     return pl.pallas_call(
         functools.partial(attend_kernel, ranks, heads),
         out_shape=jax.ShapeDtypeStruct((local_img, heads * hd), jnp.bfloat16),
-        in_specs=[vmem] * 4,
+        in_specs=[vmem] * 2,
         out_specs=pl.BlockSpec(memory_space=pl.ANY),
         scratch_shapes=[
             pltpu.VMEM((slots, ranks, local_img, hd), jnp.bfloat16),
@@ -330,7 +403,7 @@
         compiler_params=pltpu.CompilerParams(
             collective_id=1, has_side_effects=True, vmem_limit_bytes=VMEM_LIMIT
         ),
-    )(queries, keys, values, valid)
+    )(qkv, valid)
 
 
 def reduce_kernel(
@@ -465,33 +538,6 @@
     )(tile)
 
 
-def gather_features(block, size):
-    slot = lax.axis_index("tensor")
-    chips = size // 2
-    chip, core = slot // 2, lax.rem(slot, 2)
-    held = [block]
-    for hop in range(1, chips):
-        held.append(
-            lax.ppermute(
-                block, "tensor",
-                [(t, 2 * ((t // 2 + hop) % chips) + t % 2) for t in range(size)],
-            )
-        )
-    other = [lax.ppermute(b, "tensor", [(t, t ^ 1) for t in range(size)]) for b in held]
-    pairs = [
-        jnp.where(core == 0, jnp.concatenate([a, b], axis=1), jnp.concatenate([b, a], axis=1))
-        for a, b in zip(held, other)
-    ]
-    if chips == 2:
-        return jnp.where(
-            chip == 0,
-            jnp.concatenate([pairs[0], pairs[1]], axis=1),
-            jnp.concatenate([pairs[1], pairs[0]], axis=1),
-        )
-    stacked = jnp.stack(pairs)
-    return jnp.concatenate([stacked[lax.rem(chip - c + chips, chips)] for c in range(chips)], axis=1)
-
-
 def shards(
     image_states, text_states, image_qkv, text_qkv, image_out, final_weight, query_gain, key_gain,
     modulation, latent, old_velocity, rollout_noise, group_ids, text_lengths, step_ids,
@@ -503,31 +549,21 @@
     total_steps = modulation.shape[0]
     ranks = lax.axis_size("seq")
     size = lax.axis_size("tensor")
-    row_count = local_img // size
-    slot = lax.axis_index("tensor")
     group = group_ids[0]
     modrows = modulation[step_ids[0]]
     length = text_lengths[group]
     joined = jnp.concatenate([text_states[group], image_states[0]], axis=0)
-    full = gather_features(joined, size)
-    wimg = jnp.transpose(image_qkv, (1, 0, 2))
-    wtxt = jnp.transpose(text_qkv[:, 1:, :], (1, 0, 2))
-    text_f = full[:local_txt].astype(jnp.float32)
-    image_f = full[local_txt:].astype(jnp.float32)
-    normed_img = (layer_norm(image_f) * (1.0 + modrows[1]) + modrows[0]).astype(jnp.bfloat16)
-    normed_txt = (layer_norm(text_f) * (1.0 + modrows[4]) + modrows[3]).astype(jnp.bfloat16)
-    queries, keys, values = project(
-        ranks, heads, normed_img, normed_txt, wimg, wtxt, query_gain, key_gain
+    qkv, own_rows = project(
+        ranks, size, heads, local_txt, joined, modrows,
+        jnp.transpose(image_qkv, (1, 0, 2)), jnp.transpose(text_qkv, (1, 0, 2)),
+        query_gain, key_gain,
     )
     place = jnp.arange(local_txt + local_img, dtype=jnp.int32)[None, :]
     text_pos = jnp.arange(ranks, dtype=jnp.int32)[:, None] * local_txt + place
     valid = ((place >= local_txt) | (text_pos < length)).astype(jnp.float32)[:, None, :]
-    attended = attend(ranks, heads, queries, keys, values, valid)
+    attended = attend(ranks, heads, local_img, qkv, valid)
     summed = project_reduce(size, attended, image_out)
-    own_rows = lax.dynamic_slice_in_dim(
-        full, local_txt + slot * row_count, row_count, 0
-    ).astype(jnp.float32)
-    resid = own_rows + modrows[2] * summed
+    resid = own_rows.astype(jnp.float32) + modrows[2] * summed
     final_normed = (layer_norm(resid) * (1.0 + modrows[6]) + modrows[5]).astype(jnp.bfloat16)
     velocity = jnp.dot(final_normed, final_weight, preferred_element_type=jnp.float32)[None]
     flow_time, step_delta, noise_sigma, spread = plan(step_ids, total_steps)

time: 179 us -> 155 us (0.87)
  other arithmetic: 18.3 us -> 6.7 us
  waiting for transfers between devices: 10.4 us -> 0 us
  Pallas kernels: 130 us -> 137 us
  local copies, waits for them, and re-layouts: 10.6 us -> 4.36 us
  starting transfers between devices: 3.07 us -> 0 us
    ppermute x3 -> x0, waiting for transfers between devices: 10.4 us -> none  [the longest x1 10.3 us: gather_features(): lax.ppermute(block, 'tensor', [(t, 2 * ((t // 2 + hop) % chips) + t % 2)...]
    pallas_call x1, Pallas kernels: 64.4 us -> 73.1 us  [project(): pl.pallas_call(functools.partial(project_kernel, ranks, size, heads, loca...]
    transpose x1 -> x0, local copies, waits for them, and re-layouts: 7.91 us -> none  [shards(): wtxt = jnp.transpose(text_qkv[:, 1:, :], (1, 0, 2))]
    convert_element_type x2 -> x0, other arithmetic: 4.41 us -> none  [the longest x1 3.44 us: shards(): (layer_norm(image_f) * (1.0 + modrows[1]) + modrows[0]).astype(jnp.bfloat16)]
    select_n x3 -> x0, other arithmetic: 4.37 us -> none  [the longest x2 3.34 us: gather_features(): jnp.where(core == 0, jnp.concatenate([a, b], axis=1), jnp.concatenate([b,...]
    ppermute x3 -> x0, starting transfers between devices: 3.07 us -> none  [the longest x1 3.06 us: gather_features(): lax.ppermute(block, 'tensor', [(t, 2 * ((t // 2 + hop) % chips) + t % 2)...]
    reduce_sum x3 -> x1, other arithmetic: 3.07 us -> 0.4 us  [layer_norm(): row_var = jnp.mean(centred * centred, axis=-1, keepdims=True)]
  transfers between devices with their start and end apart: 3 -> 0, of which waited for: 1 -> 0; matrix products, arithmetic and copies ran while one was open for 8% -> 0% of each run, Pallas kernels for 0% -> 0%
where the time goes in v2:
time: 155 us; the launch traced here: 154 us
  Pallas kernels  137 us (88%)
  other arithmetic  6.7 us (4%)
  between operations  4.67 us (3%)
  local copies, waits for them, and re-layouts  4.36 us (3%)
  matrix products  1.82 us (1%)
    pallas_call x1, Pallas kernels, project(): pl.pallas_call(functools.partial(project_kernel, ranks, size, heads, loca...  73.1 us
    pallas_call x1, Pallas kernels, project_reduce(): pl.pallas_call(functools.partial(reduce_kernel, size), out_shape=jax.Shap...  29.3 us
    pallas_call x1, Pallas kernels, attend(): pl.pallas_call(functools.partial(attend_kernel, ranks, heads), out_shape=...  23.8 us
    pallas_call x1, Pallas kernels, total_sum(): pl.pallas_call(functools.partial(total_kernel, sizes), out_shape=jax.Shap...  10.4 us

profile of v2, /device:TPU:0, one launch (start us, length us, event | category | flops | bytes accessed | tf_op | source)
XLA Modules:
  0.0 154.2 jit_solution(621723346139648711)
XLA Ops:
  0.6 0.0 copy-start
  1.3 1.5 dynamic-slice_bitcast_fusion.mod_ref
  3.5 0.0 copy-done
  3.6 2.1 %pad_maximum_fusion.x_ref = bf16[576,768]{1,0:T(8,128)(2,1)} fusion(bf16[512,768]{1,0:T(8,128)(2,1)} %bitcast.40, bf16[64,768]{1,0:T(8,128)(2,1)S(1)} %dynamic-slice_bitcast_fusion.1), kind=kLoop, calls=%fused_computation.3 | loop fusion | flops 1769472 | bytes 1769472 | tf_op jit(solution)/shard_map/concatenate | solution.py:555
  5.7 73.1 %shard_map.158 = (bf16[2,4,576,384]{3,2,1,0:T(8,128)(2,1)}, bf16[128,3072]{1,0:T(8,128)(2,1)}) custom-call(bf16[576,768]{1,0:T(8,128)(2,1)} %pad_maximum_fusion.x_ref, f32[7,3072]{1,0:T(8,128)} %dynamic-slice_bitcast_fusion.mod_ref, bf16[3,3072,768]{2,1,0:T(8,128)(2,1)} %bitcast.38, bf16[3,3072,768]{2,1,0:T(8,128)(2,1)} %bitcast.39, f32[1,128]{1,0:T(1,128)} %bitcast.46, ...), custom_call_target="tpu_custom_call" | custom-call | tf_op jit(solution)/shard_map/pallas_call | solution.py:265
  78.8 0.6 dynamic_slice.11
  79.4 1.3 or_convert_fusion.valid_ref
  80.7 23.8 %shard_map.159.att_ref = bf16[512,768]{1,0:T(8,128)(2,1)} custom-call(bf16[2,4,576,384]{3,2,1,0:T(8,128)(2,1)} %get-tuple-element.5.qkv_ref, f32[4,1,576]{2,1,0:T(1,128)} %or_convert_fusion.valid_ref), custom_call_target="tpu_custom_call" | custom-call | tf_op jit(solution)/shard_map/pallas_call | solution.py:392
  104.5 0.0 copy-start.2
  104.5 29.3 %shard_map.160 = f32[128,3072]{1,0:T(8,128)} custom-call(bf16[512,768]{1,0:T(8,128)(2,1)} %shard_map.159.att_ref, bf16[768,3072]{1,0:T(8,128)(2,1)} %w_ref.1), custom_call_target="tpu_custom_call" | custom-call | tf_op jit(solution)/shard_map/pallas_call | solution.py:473
  133.8 1.2 constant_dynamic-slice_fusion.1
  135.0 0.0 copy-done.2
  135.0 1.7 %fusion.1 = f32[128]{0:T(128)S(1)} fusion(f32[128,3072]{1,0:T(8,128)} %shard_map.160, f32[3072]{0:T(1024)S(1)} %bitcast.41, bf16[128,3072]{1,0:T(8,128)(2,1)S(1)} %copy-done.2), kind=kLoop, calls=%fused_computation.5 | loop fusion | flops 1572736 | bytes 2372096 | tf_op jit(solution)/shard_map/reduce_sum | solution.py:16
  136.7 0.0 copy-start.4
  136.7 0.0 copy-start.5
  136.7 0.0 copy-start.6
  136.7 0.0 copy-done.1
  136.8 0.4 multiply_reduce_fusion
  137.3 0.4 copy-done.3
  137.7 0.0 copy-done.6
  137.7 1.8 %fusion.15 = (f32[]{:T(128)}, f32[1,128,64]{1,2,0:T(8,128)}) fusion(f32[1,128,64]{1,2,0:T(8,128)S(1)} %copy-done.4, f32[1,128,64]{1,2,0:T(8,128)S(1)} %copy-done.5, bf16[1,128,64]{1,2,0:T(8,128)(2,1)S(1)} %copy-done.6, f32[]{:T(128)} %bitcast.17, f32[]{:T(128)} %bitcast.15, f32[]{:T(128)} %bitcast.14, bf16[3072,64]{0,1:T(8,128)(2,1)S(1)} %copy-done.3, ...), kind=kOutput, calls=%fused_computation.25 | convolution fusion | flops 53641216 | bytes 2905104 | tf_op jit(solution)/shard_map/dot_general | solution.py:568
  140.2 0.6 broadcast_in_dim.11.x_ref
  140.7 10.4 %shard_map.161 = f32[8,128]{1,0:T(8,128)} custom-call(f32[8,128]{1,0:T(8,128)} %broadcast_in_dim.11.x_ref), custom_call_target="tpu_custom_call" | custom-call | tf_op jit(solution)/shard_map/pallas_call | solution.py:531
  151.2 1.2 slice.18
  (11 shorter events, 0.0 us)
Async XLA Ops:
  0.6 2.9 %copy-start = (bf16[4,64,768]{2,1,0:T(8,128)(2,1)S(1)}, bf16[4,64,768]{2,1,0:T(8,128)(2,1)}, u32[]{:S(2)}) copy-start(bf16[4,64,768]{2,1,0:T(8,128)(2,1)} %param.16) | copy-start | bytes 1179652
  5.7 73.1 %copy-start.7 = (s32[4]{0:T(128)S(1)}, s32[4]{0:T(128)}, u32[]{:S(2)}) copy-start(s32[4]{0:T(128)} %param.28) | copy-start | bytes 52
  104.5 30.5 %copy-start.2 = (bf16[128,3072]{1,0:T(8,128)(2,1)S(1)}, bf16[128,3072]{1,0:T(8,128)(2,1)}, u32[]{:S(2)}) copy-start(bf16[128,3072]{1,0:T(8,128)(2,1)} %get-tuple-element.4) | copy-start | bytes 2359300
  133.8 2.9 %copy-start.1 = (f32[128,3072]{1,0:T(8,128)S(1)}, f32[128,3072]{1,0:T(8,128)}, u32[]{:S(2)}) copy-start(f32[128,3072]{1,0:T(8,128)} %shard_map.160) | copy-start | bytes 4718596
  136.7 1.0 copy-start.3
  136.7 1.0 copy-start.4
  136.7 1.0 copy-start.5
  136.7 1.0 copy-start.6
